TPU v7x, 32 devices: a whole 2x2x4 slice. The times are simulated.
32 devices in a mesh: fsdp: 8 (over y, x, core), tp: 4 (over z).
Axes of the slice: x: 2, y: 2, z: 4, core: 2. Of those that a mesh axis runs over, the one named last changes fastest.
Arguments:
- emb: bfloat16 [8192, 1536], P(('fsdp', 'tp')), may hold values from -0.5 to 0.5
- segment_ids: int32 [16, 512], P('fsdp'), may hold values from 0 to 3, never falling along the last dimension, each value on 1 to 256 neighbouring positions
- routes: int32 [8192, 8], P('fsdp'), may hold values from 0 to 39, all different within a row; in each aligned block of 1024 rows (0 to 1023, 1024 to 2047, ...) at most 408 rows name the same one
- norm1_gain: bfloat16 [1536], replicated, may hold values from 0.5 to 1.5
- w_query: bfloat16 [1536, 1536], P('fsdp', 'tp'), may hold values from -0.625 to 0.625
- w_key: bfloat16 [1536, 512], P('fsdp', 'tp'), may hold values from -0.625 to 0.625
- w_value: bfloat16 [1536, 512], P('fsdp', 'tp'), may hold values from -0.15625 to 0.15625
- w_out: bfloat16 [1536, 1536], P('fsdp', 'tp'), may hold values from -1.25 to 1.25
- norm2_gain: bfloat16 [1536], replicated, may hold values from 0.5 to 1.5
- w_router: bfloat16 [1536, 40], P('fsdp'), may hold values from -0.15625 to 0.15625
- w_gate: bfloat16 [40, 1536, 512], P('tp', 'fsdp'), may hold values from -0.15625 to 0.15625
- w_up: bfloat16 [40, 1536, 512], P('tp', 'fsdp'), may hold values from -0.15625 to 0.15625
- w_down: bfloat16 [40, 1536, 512], P('tp', 'fsdp'), may hold values from -3 to 3
- cotangent: bfloat16 [8192, 1536], P(('fsdp', 'tp')), may hold values from -6 to 6
Outputs:
- out: bfloat16 [8192, 1536], P(('fsdp', 'tp'))
- grad_emb: float32 [8192, 1536], P(('fsdp', 'tp'))
- grad_norm1_gain: float32 [1536], replicated
- grad_w_query: float32 [1536, 1536], P('fsdp', 'tp')
- grad_w_key: float32 [1536, 512], P('fsdp', 'tp')
- grad_w_value: float32 [1536, 512], P('fsdp', 'tp')
- grad_w_out: float32 [1536, 1536], P('fsdp', 'tp')
- grad_norm2_gain: float32 [1536], replicated
- grad_w_router: float32 [1536, 40], P('fsdp')
- grad_w_gate: float32 [40, 1536, 512], P('tp', 'fsdp')
- grad_w_up: float32 [40, 1536, 512], P('tp', 'fsdp')
- grad_w_down: float32 [40, 1536, 512], P('tp', 'fsdp')
Inputs may be any that keep to these rules, and one draw needn't show every extreme that they name: `routes`: in each aligned block of 1024 rows no expert is named by more than 408 rows, a bound that some block reaches. `segment_ids`: along a sequence the numbers never fall; a document spans at most 256 tokens, and one spans exactly 256.
All inputs are finite; a program needn't handle non-finite values.
Results may differ from a plain program's by a relative error of at most 0.015.
Values may be sent and summed in bfloat16 or wider, within the bound.
A program may use at most 384 MiB of HBM per device.

v0:
```python
import jax
import jax.numpy as jnp
from jax import lax
from jax.sharding import PartitionSpec as P

HEAD_DIM = 64
SEQ = 512
emb_scale = 12.0
resid_scale = 0.22
attn_scale = 0.015625
norm_eps = 1e-06
rope_base = 10000.0
masked_value = -1e30


def contract_last(left_op, right_op):
    return lax.dot_general(
        left_op, right_op, (((1,), (1,)), ((), ())), preferred_element_type=jnp.float32
    )


def contract_first(left_op, right_op):
    return lax.dot_general(
        left_op, right_op, (((0,), (0,)), ((), ())), preferred_element_type=jnp.float32
    )


def rms_forward(values, gain_vec):
    inverse = lax.rsqrt(jnp.mean(values * values, axis=-1, keepdims=True) + norm_eps)
    return (values * inverse * gain_vec, inverse)


def rms_backward(incoming, values, inverse, gain_vec):
    scaled = values * inverse
    gain_grad = jnp.sum(incoming * scaled, axis=0)
    weighted = incoming * gain_vec
    row_inner = jnp.mean(weighted * scaled, axis=-1, keepdims=True)
    return (inverse * (weighted - scaled * row_inner), gain_grad)


def rotary_tables(row_count, head_width):
    half_width = head_width // 2
    positions = (jnp.arange(row_count) % SEQ).astype(jnp.float32)
    frequency = rope_base ** (-jnp.arange(half_width).astype(jnp.float32) * 2.0 / head_width)
    angles = positions[:, None] * frequency[None, :]
    return (jnp.cos(angles)[:, None, :], jnp.sin(angles)[:, None, :])


def rotate(values, cosine_table, sine_table):
    half_width = values.shape[-1] // 2
    lead_half = values[..., :half_width]
    tail_half = values[..., half_width:]
    return jnp.concatenate(
        [
            lead_half * cosine_table - tail_half * sine_table,
            tail_half * cosine_table + lead_half * sine_table,
        ],
        axis=-1,
    )


def attention_scores(queries, key_rows, segments):
    length, heads_here, head_width = queries.shape
    kv_here = key_rows.shape[1]
    grouped = queries.reshape(length, kv_here, heads_here // kv_here, head_width)
    scores = (
        jnp.einsum("qkgd,tkd->kgqt", grouped, key_rows, preferred_element_type=jnp.float32)
        * attn_scale
    )
    places = jnp.arange(length)
    allowed = (places[:, None] >= places[None, :]) & (segments[:, None] == segments[None, :])
    return (jnp.where(allowed, scores, masked_value), grouped)


def attend_forward(pieces):
    queries, key_rows, value_rows, segments = pieces
    scores, grouped = attention_scores(queries, key_rows, segments)
    row_top = jnp.max(scores, axis=-1, keepdims=True)
    raised = jnp.exp(scores - row_top)
    row_total = jnp.sum(raised, axis=-1, keepdims=True)
    probs_low = (raised / row_total).astype(jnp.bfloat16)
    mixed_out = jnp.einsum(
        "kgqt,tkd->qkgd", probs_low, value_rows, preferred_element_type=jnp.float32
    )
    return (
        mixed_out.astype(jnp.bfloat16).reshape(queries.shape[0], -1),
        (row_top + jnp.log(row_total))[..., 0],
    )


def attend_backward(pieces):
    queries, key_rows, value_rows, segments, logsum, mixed_grad = pieces
    scores, grouped = attention_scores(queries, key_rows, segments)
    attn_probs = jnp.exp(scores - logsum[..., None])
    grad_grouped = mixed_grad.reshape(grouped.shape)
    probs_grad = jnp.einsum(
        "qkgd,tkd->kgqt", grad_grouped, value_rows, preferred_element_type=jnp.float32
    )
    row_inner = jnp.sum(attn_probs * probs_grad, axis=-1, keepdims=True)
    score_grad = (attn_probs * (probs_grad - row_inner)).astype(jnp.bfloat16)
    query_grad = (
        jnp.einsum("kgqt,tkd->qkgd", score_grad, key_rows, preferred_element_type=jnp.float32)
        * attn_scale
    )
    key_grad = (
        jnp.einsum("kgqt,qkgd->tkd", score_grad, grouped, preferred_element_type=jnp.float32)
        * attn_scale
    )
    value_grad = jnp.einsum(
        "kgqt,qkgd->tkd",
        attn_probs.astype(jnp.bfloat16),
        grad_grouped,
        preferred_element_type=jnp.float32,
    )
    return (query_grad.reshape(queries.shape), key_grad, value_grad)


def route_slots(expert, group_routes, group_gates, capacity):
    hit_mask = group_routes == expert
    member = jnp.any(hit_mask, axis=1)
    weight = jnp.sum(jnp.where(hit_mask, group_gates.astype(jnp.float32), 0.0), axis=1)
    member_int = member.astype(jnp.int32)
    slot_index = jnp.cumsum(member_int) - 1
    target = jnp.where(member, slot_index, capacity)
    row_ids = jnp.arange(member.shape[0], dtype=jnp.int32)
    slot_rows = jnp.zeros((capacity,), jnp.int32).at[target].set(row_ids, mode="drop")
    filled = jnp.arange(capacity) < jnp.sum(member_int)
    slot_scale = jnp.where(filled, jnp.take(weight, slot_rows, axis=0), 0.0)
    picked = jnp.where(filled[:, None], jnp.take(hit_mask, slot_rows, axis=0), False).astype(
        jnp.float32
    )
    return (slot_rows, slot_scale, picked)


def local(
    emb,
    segment_ids,
    routes,
    norm1_gain,
    w_query,
    w_key,
    w_value,
    w_out,
    norm2_gain,
    w_router,
    w_gate,
    w_up,
    w_down,
    cotangent,
):
    local_rows = emb.shape[0]
    query_w, key_w, value_w, out_w, router_w, gate_w, up_w, down_w = (
        lax.all_gather(w_query, "fsdp", axis=0, tiled=True),
        lax.all_gather(w_key, "fsdp", axis=0, tiled=True),
        lax.all_gather(w_value, "fsdp", axis=0, tiled=True),
        lax.all_gather(w_out, "fsdp", axis=0, tiled=True),
        lax.all_gather(w_router, "fsdp", axis=0, tiled=True),
        lax.all_gather(w_gate, "fsdp", axis=1, tiled=True),
        lax.all_gather(w_up, "fsdp", axis=1, tiled=True),
        lax.all_gather(w_down, "fsdp", axis=1, tiled=True),
    )
    gain_one = norm1_gain.astype(jnp.float32)
    gain_two = norm2_gain.astype(jnp.float32)
    start_x = emb.astype(jnp.float32) * emb_scale
    normed_one, inverse_one = rms_forward(start_x, gain_one)
    group_rows = lax.all_gather(normed_one.astype(jnp.bfloat16), "tp", axis=0, tiled=True)
    group_size = group_rows.shape[0]
    seq_count = group_size // SEQ
    heads_here = query_w.shape[1] // HEAD_DIM
    kv_here = key_w.shape[1] // HEAD_DIM
    cosine_table, sine_table = rotary_tables(group_size, HEAD_DIM)
    query_proj = jnp.dot(group_rows, query_w, preferred_element_type=jnp.float32).reshape(
        group_size, heads_here, HEAD_DIM
    )
    key_proj = jnp.dot(group_rows, key_w, preferred_element_type=jnp.float32).reshape(
        group_size, kv_here, HEAD_DIM
    )
    queries = rotate(query_proj, cosine_table, sine_table).astype(jnp.bfloat16)
    key_rows = rotate(key_proj, cosine_table, sine_table).astype(jnp.bfloat16)
    value_rows = jnp.dot(group_rows, value_w, preferred_element_type=jnp.float32).astype(
        jnp.bfloat16
    )
    seq_queries = queries.reshape(seq_count, SEQ, heads_here, HEAD_DIM)
    seq_keys = key_rows.reshape(seq_count, SEQ, kv_here, HEAD_DIM)
    seq_values = value_rows.reshape(seq_count, SEQ, kv_here, HEAD_DIM)
    mixed_out, logsum = lax.map(attend_forward, (seq_queries, seq_keys, seq_values, segment_ids))
    mixed_rows = mixed_out.reshape(group_size, heads_here * HEAD_DIM)
    attn_branch = lax.psum_scatter(
        contract_last(mixed_rows, out_w), "tp", scatter_dimension=0, tiled=True
    )
    mid_x = start_x + resid_scale * attn_branch
    normed_two, inverse_two = rms_forward(mid_x, gain_two)
    normed_low = normed_two.astype(jnp.bfloat16)
    logits = jnp.dot(normed_low, router_w, preferred_element_type=jnp.float32)
    tp_index = lax.axis_index("tp")
    own_routes = lax.dynamic_slice_in_dim(routes, tp_index * local_rows, local_rows, 0)
    expert_count = router_w.shape[1]
    chosen = (own_routes[:, :, None] == jnp.arange(expert_count)[None, None, :]).astype(jnp.float32)
    selected = jnp.sum(chosen * logits[:, None, :], axis=-1)
    sel_top = jnp.max(selected, axis=-1, keepdims=True)
    sel_raised = jnp.exp(selected - sel_top)
    gates = sel_raised / jnp.sum(sel_raised, axis=-1, keepdims=True)
    moe_rows, group_gates = (
        lax.all_gather(normed_low, "tp", axis=0, tiled=True),
        lax.all_gather(gates.astype(jnp.bfloat16), "tp", axis=0, tiled=True),
    )
    experts_here = gate_w.shape[0]
    capacity = group_size * routes.shape[1] // expert_count * 2
    expert_ids = tp_index * experts_here + jnp.arange(experts_here, dtype=jnp.int32)

    def expert_forward(running, inputs):
        gate_one, up_one, down_one, expert = inputs
        slot_rows, slot_scale, picked = route_slots(expert, routes, group_gates, capacity)
        rows_taken = jnp.take(moe_rows, slot_rows, axis=0)
        gate_pre = jnp.dot(rows_taken, gate_one, preferred_element_type=jnp.float32)
        up_pre = jnp.dot(rows_taken, up_one, preferred_element_type=jnp.float32)
        act_low = (gate_pre * jax.nn.sigmoid(gate_pre) * up_pre).astype(jnp.bfloat16)
        expert_out = contract_last(act_low, down_one)
        running = running.at[slot_rows].add(expert_out * slot_scale[:, None])
        return (running, (slot_rows, slot_scale, picked, gate_pre, up_pre, act_low, expert_out))

    moe_start = jnp.zeros((group_size, moe_rows.shape[1]), jnp.float32)
    moe_part, kept = lax.scan(expert_forward, moe_start, (gate_w, up_w, down_w, expert_ids))
    moe_sum = lax.psum_scatter(moe_part, "tp", scatter_dimension=0, tiled=True)
    out = (mid_x + resid_scale * moe_sum).astype(jnp.bfloat16)
    out_grad = cotangent.astype(jnp.float32)
    moe_grad = (resid_scale * out_grad).astype(jnp.bfloat16)
    moe_grad_rows = lax.all_gather(moe_grad, "tp", axis=0, tiled=True)
    gate_back, up_back, down_back = (gate_w, up_w, down_w)

    def expert_backward(running, inputs):
        rows_grad, gates_part = running
        (
            gate_one,
            up_one,
            down_one,
            slot_rows,
            slot_scale,
            picked,
            gate_pre,
            up_pre,
            act_low,
            expert_out,
        ) = inputs
        rows_taken = jnp.take(moe_rows, slot_rows, axis=0)
        taken_grad = jnp.take(moe_grad_rows, slot_rows, axis=0).astype(jnp.float32)
        slot_grad = jnp.sum(expert_out * taken_grad, axis=1)
        gates_part = gates_part.at[slot_rows].add(picked * slot_grad[:, None])
        scaled_grad = (taken_grad * slot_scale[:, None]).astype(jnp.bfloat16)
        down_grad = contract_first(scaled_grad, act_low)
        act_grad = jnp.dot(scaled_grad, down_one, preferred_element_type=jnp.float32)
        sig_gate = jax.nn.sigmoid(gate_pre)
        gate_grad = (act_grad * up_pre * sig_gate * (1.0 + gate_pre * (1.0 - sig_gate))).astype(
            jnp.bfloat16
        )
        up_grad = (act_grad * gate_pre * sig_gate).astype(jnp.bfloat16)
        gate_w_grad = contract_first(rows_taken, gate_grad)
        up_w_grad = contract_first(rows_taken, up_grad)
        input_grad = contract_last(gate_grad, gate_one) + contract_last(up_grad, up_one)
        rows_grad = rows_grad.at[slot_rows].add(input_grad)
        return ((rows_grad, gates_part), (gate_w_grad, up_w_grad, down_grad))

    back_start = (
        jnp.zeros((group_size, moe_rows.shape[1]), jnp.float32),
        jnp.zeros((group_size, routes.shape[1]), jnp.float32),
    )
    (rows_grad_part, gates_grad_part), (gate_grads, up_grads, down_grads) = lax.scan(
        expert_backward, back_start, (gate_back, up_back, down_back) + kept
    )
    rows_grad_sum, gates_grad = (
        lax.psum_scatter(rows_grad_part, "tp", scatter_dimension=0, tiled=True),
        lax.psum_scatter(gates_grad_part, "tp", scatter_dimension=0, tiled=True),
    )
    gates_inner = jnp.sum(gates * gates_grad, axis=-1, keepdims=True)
    selected_grad = gates * (gates_grad - gates_inner)
    logits_grad = jnp.sum(chosen * selected_grad[:, :, None], axis=1).astype(jnp.bfloat16)
    router_grad_part = contract_first(normed_low, logits_grad)
    normed_two_grad = rows_grad_sum + contract_last(logits_grad, router_w)
    mid_from_norm, gain_two_grad = rms_backward(normed_two_grad, mid_x, inverse_two, gain_two)
    mid_grad = out_grad + mid_from_norm
    branch_grad = (resid_scale * mid_grad).astype(jnp.bfloat16)
    branch_grad_rows = lax.all_gather(branch_grad, "tp", axis=0, tiled=True)
    out_w_grad = contract_first(branch_grad_rows, mixed_rows)
    mixed_grad = jnp.dot(branch_grad_rows, out_w, preferred_element_type=jnp.float32).astype(
        jnp.bfloat16
    )
    query_grad, key_grad, value_grad = lax.map(
        attend_backward,
        (
            seq_queries,
            seq_keys,
            seq_values,
            segment_ids,
            logsum,
            mixed_grad.reshape(seq_count, SEQ, -1),
        ),
    )
    query_proj_grad = (
        rotate(query_grad.reshape(group_size, heads_here, HEAD_DIM), cosine_table, -sine_table)
        .astype(jnp.bfloat16)
        .reshape(group_size, -1)
    )
    key_proj_grad = (
        rotate(key_grad.reshape(group_size, kv_here, HEAD_DIM), cosine_table, -sine_table)
        .astype(jnp.bfloat16)
        .reshape(group_size, -1)
    )
    value_proj_grad = value_grad.reshape(group_size, -1).astype(jnp.bfloat16)
    query_w_grad = contract_first(group_rows, query_proj_grad)
    key_w_grad = contract_first(group_rows, key_proj_grad)
    value_w_grad = contract_first(group_rows, value_proj_grad)
    total_grad = contract_last(query_proj_grad, query_w)
    total_grad = total_grad + contract_last(key_proj_grad, key_w)
    normed_one_grad = lax.psum_scatter(
        total_grad + contract_last(value_proj_grad, value_w), "tp", scatter_dimension=0, tiled=True
    )
    start_from_norm, gain_one_grad = rms_backward(normed_one_grad, start_x, inverse_one, gain_one)
    grad_emb = emb_scale * (mid_grad + start_from_norm)
    gain_one_sum, gain_two_sum, router_sum = lax.psum(
        (gain_one_grad, gain_two_grad, router_grad_part), ("fsdp", "tp")
    )
    router_rows = w_router.shape[0]
    router_own = lax.dynamic_slice_in_dim(
        router_sum, lax.axis_index("fsdp") * router_rows, router_rows, 0
    )
    query_sum, key_sum, value_sum, out_sum = (
        lax.psum_scatter(query_w_grad, "fsdp", scatter_dimension=0, tiled=True),
        lax.psum_scatter(key_w_grad, "fsdp", scatter_dimension=0, tiled=True),
        lax.psum_scatter(value_w_grad, "fsdp", scatter_dimension=0, tiled=True),
        lax.psum_scatter(out_w_grad, "fsdp", scatter_dimension=0, tiled=True),
    )
    gate_sum, up_sum, down_sum = (
        lax.psum_scatter(gate_grads, "fsdp", scatter_dimension=1, tiled=True),
        lax.psum_scatter(up_grads, "fsdp", scatter_dimension=1, tiled=True),
        lax.psum_scatter(down_grads, "fsdp", scatter_dimension=1, tiled=True),
    )
    return (
        out,
        grad_emb,
        gain_one_sum,
        query_sum,
        key_sum,
        value_sum,
        out_sum,
        gain_two_sum,
        router_own,
        gate_sum,
        up_sum,
        down_sum,
    )


def solution(mesh):
    return jax.shard_map(
        local,
        mesh=mesh,
        in_specs=(
            P(("fsdp", "tp"), None),
            P("fsdp", None),
            P("fsdp", None),
            P(),
            P("fsdp", "tp"),
            P("fsdp", "tp"),
            P("fsdp", "tp"),
            P("fsdp", "tp"),
            P(),
            P("fsdp", None),
            P("tp", "fsdp", None),
            P("tp", "fsdp", None),
            P("tp", "fsdp", None),
            P(("fsdp", "tp"), None),
        ),
        out_specs=(
            P(("fsdp", "tp"), None),
            P(("fsdp", "tp"), None),
            P(),
            P("fsdp", "tp"),
            P("fsdp", "tp"),
            P("fsdp", "tp"),
            P("fsdp", "tp"),
            P(),
            P("fsdp", None),
            P("tp", "fsdp", None),
            P("tp", "fsdp", None),
            P("tp", "fsdp", None),
        ),
        check_vma=False,
    )
```

profile of v0, /device:TPU:0, one launch (start us, length us, event | category | flops | bytes accessed | tf_op | source)
XLA Modules:
  0.0 2862.0 jit_solution(5613374487226321994)
XLA Ops:
  37.2 41.9 %all-gather.11.cloned.1.call-done = bf16[1024,1536]{1,0:T(8,128)(2,1)} async-done(((bf16[256,1536]{1,0:T(8,128)(2,1)}), bf16[1024,1536]{1,0:T(8,128)(2,1)}) %all-gather.11.cloned.1.call-update) | async-done | bytes 3145744 | tf_op jit(solution)/shard_map/all_gather | solution.py:166
  89.1 14.5 all-gather.13.cloned.1.call-done
  108.3 13.1 while.70
  136.1 110.3 %reduce-scatter.13.cloned.1.call-done = f32[256,1536]{1,0:T(8,128)} async-done(((f32[1024,1536]{1,0:T(8,128)}), f32[256,1536]{1,0:T(8,128)}) %reduce-scatter.13.cloned.1.call-update) | async-done | bytes 1572880 | tf_op jit(solution)/shard_map/reduce_scatter | solution.py:188
  266.1 14.2 all_gather.49
  280.6 34.2 %all-gather.17.cloned.1.call-done = bf16[1024,1536]{1,0:T(8,128)(2,1)} async-done(((bf16[256,1536]{1,0:T(8,128)(2,1)}), bf16[1024,1536]{1,0:T(8,128)(2,1)}) %all-gather.17.cloned.1.call-update) | async-done | bytes 3145744 | tf_op jit(solution)/shard_map/all_gather | solution.py:204
  314.8 85.7 %all-gather.19.cloned.1.call-done = bf16[10,1536,512]{2,1,0:T(8,128)(2,1)} async-done(((bf16[10,192,512]{2,1,0:T(8,128)(2,1)}), bf16[10,1536,512]{2,1,0:T(8,128)(2,1)}) %all-gather.19.cloned.1.call-update) | async-done | bytes 15728656 | tf_op jit(solution)/shard_map/all_gather | solution.py:158
  400.5 87.2 %all-gather.21.cloned.1.call-done = bf16[10,1536,512]{2,1,0:T(8,128)(2,1)} async-done(((bf16[10,192,512]{2,1,0:T(8,128)(2,1)}), bf16[10,1536,512]{2,1,0:T(8,128)(2,1)}) %all-gather.21.cloned.1.call-update) | async-done | bytes 15728656 | tf_op jit(solution)/shard_map/all_gather | solution.py:159
  487.8 87.2 %all-gather.23.cloned.1.call-done = bf16[10,1536,512]{2,1,0:T(8,128)(2,1)} async-done(((bf16[10,192,512]{2,1,0:T(8,128)(2,1)}), bf16[10,1536,512]{2,1,0:T(8,128)(2,1)}) %all-gather.23.cloned.1.call-update) | async-done | bytes 15728656 | tf_op jit(solution)/shard_map/all_gather | solution.py:160
  578.4 468.3 %while.71 = (s32[]{:T(128)}, f32[1024,1536]{1,0:T(8,128)}, s32[10,408]{1,0:T(8,128)}, f32[10,408]{1,0:T(8,128)}, f32[10,408,8]{2,1,0:T(8,128)}, /*index=5*/f32[1...) while((s32[]{:T(128)}, f32[1024,1536]{1,0:T(8,128)}, ...), condition=%wide.region_18.20_spmd, body=%wide.region_10.19_spmd.sunk | while | flops 1929139968 | bytes 35207396 | solution.py:223
  614.2 11.3 scatter_custom_fusion.17
  661.0 11.2 scatter_custom_fusion.17
  707.9 11.2 scatter_custom_fusion.17
  754.7 11.2 scatter_custom_fusion.17
  1050.9 505.1 %while.72 = (s32[]{:T(128)}, f32[1024,1536]{1,0:T(8,128)}, f32[1024,8]{1,0:T(8,128)}, f32[10,1536,512]{2,1,0:T(8,128)}, f32[10,1536,512]{2,1,0:T(8,128)}, /*inde...) while((s32[]{:T(128)}, f32[1024,1536]{1,0:T(8,128)}, ...), condition=%wide.region_24.26_spmd, body=%wide.region_20.25_spmd.sunk | while | flops 3863125760 | bytes 57883772 | solution.py:267
  1558.7 18.9 reduce-scatter.19.cloned.1.call-done
  1579.1 109.7 %reduce-scatter.17.cloned.1.call-done = f32[256,1536]{1,0:T(8,128)} async-done(((f32[1024,1536]{1,0:T(8,128)}), f32[256,1536]{1,0:T(8,128)}) %reduce-scatter.17.cloned.1.call-update) | async-done | bytes 1572880 | tf_op jit(solution)/shard_map/reduce_scatter | solution.py:271
  1694.7 63.0 %all-gather.27.cloned.1.call-done = bf16[1024,1536]{1,0:T(8,128)(2,1)} async-done(((bf16[256,1536]{1,0:T(8,128)(2,1)}), bf16[1024,1536]{1,0:T(8,128)(2,1)}) %all-gather.27.cloned.1.call-update) | async-done | bytes 3145744 | tf_op jit(solution)/shard_map/all_gather | solution.py:282
  1762.5 65.1 %while.73 = (s32[]{:T(128)}, f32[2,512,6,64]{1,0,3,2:T(2,128)}, f32[2,512,2,64]{1,0,3,2:T(2,128)}, bf16[2,512,2,64]{1,3,2,0:T(8,128)(2,1)}, bf16[2,512,2,64]{1,3...) while((s32[]{:T(128)}, f32[2,512,6,64]{1,0,3,2:T(2,128)}, ...), condition=%wide.region_32.34_spmd, body=%wide.region_30.33_spmd.sunk | while | flops 1031271424 | bytes 58161316 | solution.py:287
  1780.1 15.0 dynamic_update_slice.116
  1812.6 15.0 dynamic_update_slice.116
  1860.1 27.0 all-reduce.3.cloned.1.call-done
  1888.6 111.7 %reduce-scatter.21.cloned.1.call-done = f32[256,1536]{1,0:T(8,128)} async-done(((f32[1024,1536]{1,0:T(8,128)}), f32[256,1536]{1,0:T(8,128)}) %reduce-scatter.21.cloned.1.call-update) | async-done | bytes 1572880 | tf_op jit(solution)/shard_map/reduce_scatter | solution.py:314
  2002.3 45.1 %all-reduce = (f32[1536]{0:T(1024)}, f32[1536]{0:T(1024)}) all-reduce(f32[1536]{0:T(1024)S(1)} %get-tuple-element.575, f32[1536]{0:T(1024)S(1)} %get-tuple-element.573), channel_id=1, replica_groups=mesh['fsdp'=8,'tp'=4] {'fsdp','tp'}, use_global_device_ids=true, to_apply=%region_36.38 | all-reduce | flops 3072 | bytes 24576 | tf_op jit(solution)/shard_map/psum | solution.py:319
  2047.3 67.5 %reduce-scatter.15.cloned.1.call-done = f32[256,1536]{1,0:T(8,128)} async-done(((f32[1024,1536]{1,0:T(8,128)}), f32[256,1536]{1,0:T(8,128)}) %reduce-scatter.15.cloned.1.call-update) | async-done | bytes 1572880 | tf_op jit(solution)/shard_map/reduce_scatter | solution.py:224
  2119.5 34.4 %reduce-scatter.25.cloned.1.call-done = f32[192,128]{1,0:T(8,128)} async-done(((f32[1536,128]{1,0:T(8,128)}), f32[192,128]{1,0:T(8,128)}) %reduce-scatter.25.cloned.1.call-update) | async-done | bytes 98320 | tf_op jit(solution)/shard_map/reduce_scatter | solution.py:328
  2153.9 38.6 %reduce-scatter.27.cloned.1.call-done = f32[192,128]{1,0:T(8,128)} async-done(((f32[1536,128]{1,0:T(8,128)}), f32[192,128]{1,0:T(8,128)}) %reduce-scatter.27.cloned.1.call-update) | async-done | bytes 98320 | tf_op jit(solution)/shard_map/reduce_scatter | solution.py:329
  2192.5 46.2 %reduce-scatter.29.cloned.1.call-done = f32[192,384]{1,0:T(8,128)} async-done(((f32[1536,384]{1,0:T(8,128)}), f32[192,384]{1,0:T(8,128)}) %reduce-scatter.29.cloned.1.call-update) | async-done | bytes 294928 | tf_op jit(solution)/shard_map/reduce_scatter | solution.py:330
  2238.7 46.3 %reduce-scatter.23.cloned.1.call-done = f32[192,384]{1,0:T(8,128)} async-done(((f32[1536,384]{1,0:T(8,128)}), f32[192,384]{1,0:T(8,128)}) %reduce-scatter.23.cloned.1.call-update) | async-done | bytes 294928 | tf_op jit(solution)/shard_map/reduce_scatter | solution.py:327
  2284.9 189.9 %reduce-scatter.35.cloned.1.call-done = f32[10,192,512]{2,1,0:T(8,128)} async-done(((f32[10,1536,512]{2,1,0:T(8,128)}), f32[10,192,512]{2,1,0:T(8,128)}) %reduce-scatter.35.cloned.1.call-update) | async-done | bytes 3932176 | tf_op jit(solution)/shard_map/reduce_scatter | solution.py:335
  2474.8 190.1 %reduce-scatter.31.cloned.1.call-done = f32[10,192,512]{2,1,0:T(8,128)} async-done(((f32[10,1536,512]{2,1,0:T(8,128)}), f32[10,192,512]{2,1,0:T(8,128)}) %reduce-scatter.31.cloned.1.call-update) | async-done | bytes 3932176 | tf_op jit(solution)/shard_map/reduce_scatter | solution.py:333
  2664.9 190.0 %reduce-scatter.33.cloned.1.call-done = f32[10,192,512]{2,1,0:T(8,128)} async-done(((f32[10,1536,512]{2,1,0:T(8,128)}), f32[10,192,512]{2,1,0:T(8,128)}) %reduce-scatter.33.cloned.1.call-update) | async-done | bytes 3932176 | tf_op jit(solution)/shard_map/reduce_scatter | solution.py:334
  (944 shorter events, 1115.9 us)
Async XLA Ops:
  7.2 71.9 %all-gather.11.cloned.1.call-start = ((), (), s32[]{:S(2)}) async-start(), calls=%async_computation.12 | async-start | bytes 3932160 | tf_op jit(solution)/shard_map/all_gather | solution.py:166
  12.8 90.8 %all-gather.13.cloned.1.call-start = ((), (), s32[]{:S(2)}) async-start(), calls=%async_computation.13 | async-start | bytes 1327104 | tf_op jit(solution)/shard_map/all_gather | solution.py:153
  13.5 115.9 %all-gather.15.cloned.1.call-start = ((), (), s32[]{:S(2)}) async-start(), calls=%async_computation.14 | async-start | bytes 1327104 | tf_op jit(solution)/shard_map/all_gather | solution.py:156
  14.3 232.1 %reduce-scatter.13.cloned.1.call-start = ((), (), s32[]{:S(2)}) async-start(), calls=%async_computation.15 | async-start | bytes 7864320 | tf_op jit(solution)/shard_map/reduce_scatter | solution.py:188
  135.5 179.3 %all-gather.17.cloned.1.call-start = ((), (), s32[]{:S(2)}) async-start(), calls=%async_computation.16 | async-start | bytes 3932160 | tf_op jit(solution)/shard_map/all_gather | solution.py:204
  250.5 150.0 %all-gather.19.cloned.1.call-start = ((), (), s32[]{:S(2)}) async-start(), calls=%async_computation.17 | async-start | bytes 17694720 | tf_op jit(solution)/shard_map/all_gather | solution.py:158
  251.1 236.7 %all-gather.21.cloned.1.call-start = ((), (), s32[]{:S(2)}) async-start(), calls=%async_computation.18 | async-start | bytes 17694720 | tf_op jit(solution)/shard_map/all_gather | solution.py:159
  251.9 323.1 %all-gather.23.cloned.1.call-start = ((), (), s32[]{:S(2)}) async-start(), calls=%async_computation.19 | async-start | bytes 17694720 | tf_op jit(solution)/shard_map/all_gather | solution.py:160
  252.6 794.1 %all-gather.25.cloned.1.call-start = ((), (), s32[]{:S(2)}) async-start(), calls=%async_computation.21 | async-start | bytes 3932160 | tf_op jit(solution)/shard_map/all_gather | solution.py:228
  253.7 1323.9 %reduce-scatter.19.cloned.1.call-start = ((), (), s32[]{:S(2)}) async-start(), calls=%async_computation.23 | async-start | bytes 40960 | tf_op jit(solution)/shard_map/reduce_scatter | solution.py:272
  314.8 263.6 %copy-start = (bf16[1024,1536]{1,0:T(8,128)(2,1)S(1)}, bf16[1024,1536]{1,0:T(8,128)(2,1)}, u32[]{:S(2)}) copy-start(bf16[1024,1536]{1,0:T(8,128)(2,1)} %all-gather.17.cloned.1.call-done) | copy-start | bytes 9437188
  1557.9 130.9 %reduce-scatter.17.cloned.1.call-start = ((), (), s32[]{:S(2)}) async-start(), calls=%async_computation.22 | async-start | bytes 7864320 | tf_op jit(solution)/shard_map/reduce_scatter | solution.py:271
  1558.0 130.8 %copy-start.4 = (f32[256,1536]{1,0:T(8,128)S(1)}, f32[256,1536]{1,0:T(8,128)}, u32[]{:S(2)}) copy-start(f32[256,1536]{1,0:T(8,128)} %copy-done.3) | copy-start | bytes 4718596
  1558.0 130.8 %copy-start.41 = (bf16[1536,40]{0,1:T(8,128)(2,1)S(1)}, bf16[1536,40]{0,1:T(8,128)(2,1)}, u32[]{:S(2)}) copy-start(bf16[1536,40]{0,1:T(8,128)(2,1)} %copy-done.40) | copy-start | bytes 368644
  1558.6 133.4 %copy-start.21 = (bf16[256,1536]{1,0:T(8,128)(2,1)S(1)}, bf16[256,1536]{1,0:T(8,128)(2,1)}, u32[]{:S(2)}) copy-start(bf16[256,1536]{1,0:T(8,128)(2,1)} %param.37) | copy-start | bytes 2359300
  1558.6 199.0 %all-gather.27.cloned.1.call-start = ((), (), s32[]{:S(2)}) async-start(), calls=%async_computation.24 | async-start | bytes 3932160 | tf_op jit(solution)/shard_map/all_gather | solution.py:282
  1693.5 193.6 %all-reduce.3.cloned.1.call-start = ((), (), s32[]{:S(2)}) async-start(), calls=%async_computation.30 | async-start | bytes 491520 | tf_op jit(solution)/shard_map/psum | solution.py:319
  1694.6 305.7 %reduce-scatter.21.cloned.1.call-start = ((), (), s32[]{:S(2)}) async-start(), calls=%async_computation.25 | async-start | bytes 7864320 | tf_op jit(solution)/shard_map/reduce_scatter | solution.py:314
  1841.3 273.5 %reduce-scatter.15.cloned.1.call-start = ((), (), s32[]{:S(2)}) async-start(), calls=%async_computation.20 | async-start | bytes 7864320 | tf_op jit(solution)/shard_map/reduce_scatter | solution.py:224
  1841.9 312.0 %reduce-scatter.25.cloned.1.call-start = ((), (), s32[]{:S(2)}) async-start(), calls=%async_computation.27 | async-start | bytes 884736 | tf_op jit(solution)/shard_map/reduce_scatter | solution.py:328
  1845.2 347.3 %reduce-scatter.27.cloned.1.call-start = ((), (), s32[]{:S(2)}) async-start(), calls=%async_computation.28 | async-start | bytes 884736 | tf_op jit(solution)/shard_map/reduce_scatter | solution.py:329
  1848.1 390.6 %reduce-scatter.29.cloned.1.call-start = ((), (), s32[]{:S(2)}) async-start(), calls=%async_computation.29 | async-start | bytes 2654208 | tf_op jit(solution)/shard_map/reduce_scatter | solution.py:330
  1853.5 431.5 %reduce-scatter.23.cloned.1.call-start = ((), (), s32[]{:S(2)}) async-start(), calls=%async_computation.26 | async-start | bytes 2654208 | tf_op jit(solution)/shard_map/reduce_scatter | solution.py:327
  1858.0 616.9 %reduce-scatter.35.cloned.1.call-start = ((), (), s32[]{:S(2)}) async-start(), calls=%async_computation.33 | async-start | bytes 35389440 | tf_op jit(solution)/shard_map/reduce_scatter | solution.py:335
  1858.6 806.3 %reduce-scatter.31.cloned.1.call-start = ((), (), s32[]{:S(2)}) async-start(), calls=%async_computation.31 | async-start | bytes 35389440 | tf_op jit(solution)/shard_map/reduce_scatter | solution.py:333
  1859.3 995.6 %reduce-scatter.33.cloned.1.call-start = ((), (), s32[]{:S(2)}) async-start(), calls=%async_computation.32 | async-start | bytes 35389440 | tf_op jit(solution)/shard_map/reduce_scatter | solution.py:334
  1859.3 141.0 %copy-start.13 = (bf16[256,1536]{1,0:T(8,128)(2,1)S(1)}, bf16[256,1536]{1,0:T(8,128)(2,1)}, u32[]{:S(2)}) copy-start(bf16[256,1536]{1,0:T(8,128)(2,1)} %param.24) | copy-start | bytes 2359300
  1859.3 141.0 %copy-start.49 = (f32[1536]{0:T(1024)S(1)}, f32[1536]{0:T(1024)}, u32[]{:S(2)}) copy-start(f32[1536]{0:T(1024)} %copy-done.48) | copy-start | bytes 18436
  1859.4 141.0 %copy-start.65 = (f32[256]{0:T(256)S(1)}, f32[256]{0:T(256)}, u32[]{:S(2)}) copy-start(f32[256]{0:T(256)} %copy-done.64) | copy-start | bytes 3076
  1859.4 255.5 %copy-start.67 = (f32[256]{0:T(256)S(1)}, f32[256]{0:T(256)}, u32[]{:S(2)}) copy-start(f32[256]{0:T(256)} %get-tuple-element.715) | copy-start | bytes 3076
  1860.0 254.8 %copy-start.5 = (f32[256,1536]{1,0:T(8,128)S(1)}, f32[256,1536]{1,0:T(8,128)}, u32[]{:S(2)}) copy-start(f32[256,1536]{1,0:T(8,128)} %copy-done.3) | copy-start | bytes 4718596
  1860.0 254.8 %copy-start.22 = (bf16[256,1536]{1,0:T(8,128)(2,1)S(1)}, bf16[256,1536]{1,0:T(8,128)(2,1)}, u32[]{:S(2)}) copy-start(bf16[256,1536]{1,0:T(8,128)(2,1)} %param.37) | copy-start | bytes 2359300
  (153 other events, 1550.3 us)
Sparse Core Ops, SparseCore 0:
  12.9 66.1 all-gather.10
  81.0 22.5 all-gather.12
  105.5 23.9 all-gather.14
  135.6 110.7 reduce-scatter.12
  250.6 64.1 all-gather.16
  316.5 83.9 all-gather.18
  402.4 85.2 all-gather.20
  489.6 85.2 all-gather.22
  577.1 63.4 all-gather.24
  1558.0 19.4 reduce-scatter.18
  1579.9 108.8 reduce-scatter.16
  1693.6 63.9 all-gather.26
  1763.1 123.8 all-reduce.2
  1889.2 111.0 reduce-scatter.20
  2002.5 112.3 reduce-scatter.14
  2118.4 35.4 reduce-scatter.24
  2157.5 34.9 reduce-scatter.26
  2196.2 42.3 reduce-scatter.28
  2242.6 42.3 reduce-scatter.22
  2289.0 185.8 reduce-scatter.34
  2479.0 185.8 reduce-scatter.30
  2669.1 185.7 reduce-scatter.32
where the time goes:
time: 2880 us; the launch traced here: 2860 us
  waiting for transfers between devices  1610 us (56%)
  other arithmetic  412 us (14%)
  matrix products  385 us (13%)
  local copies, waits for them, and re-layouts  348 us (12%)
  blocking collectives  90.3 us (3%)
    reduce_scatter x1, waiting for transfers between devices, local(): lax.psum_scatter(gate_grads, 'fsdp', scatter_dimension=1, tiled=True)  190 us
    reduce_scatter x1, waiting for transfers between devices, local(): lax.psum_scatter(up_grads, 'fsdp', scatter_dimension=1, tiled=True)  190 us
    reduce_scatter x1, waiting for transfers between devices, local(): lax.psum_scatter(down_grads, 'fsdp', scatter_dimension=1, tiled=True)  190 us
    dot_general x35, matrix products, contract_last(): lax.dot_general(left_op, right_op, (((1,), (1,)), ((), ())), preferred_el...  122 us
    dot_general x35, matrix products, contract_first(): lax.dot_general(left_op, right_op, (((0,), (0,)), ((), ())), preferred_el...  117 us
    scatter-add x10, other arithmetic, expert_forward(): running = running.at[slot_rows].add(expert_out * slot_scale[:, None])  112 us
    reduce_scatter x1, waiting for transfers between devices, local(): lax.psum_scatter(total_grad + contract_last(value_proj_grad, value_w), 't...  112 us
    reduce_scatter x1, waiting for transfers between devices, local(): lax.psum_scatter(contract_last(mixed_rows, out_w), 'tp', scatter_dimensio...  110 us
  transfers between devices with their start and end apart: 22, of which 21 were waited for; matrix products, arithmetic and copies ran while one was open for 21% of the time, Pallas kernels for 0%

commit v1 on v0

--- a/solution.py
+++ b/solution.py
@@ -2,6 +2,7 @@
 import jax.numpy as jnp
 from jax import lax
 from jax.sharding import PartitionSpec as P
+from jax.lax import axis_index, axis_size, ppermute
 
 HEAD_DIM = 64
 SEQ = 512
@@ -11,6 +12,28 @@
 norm_eps = 1e-06
 rope_base = 10000.0
 masked_value = -1e30
+
+
+def _build_tracks(x_local, d_out):
+    vec_out = list(x_local.shape[1:])
+    vec_out[d_out] *= x_local.shape[0]
+    return jnp.moveaxis(x_local, 0, d_out).reshape(vec_out)
+
+
+def answer_masks(packet, row_axis):
+    block_out = axis_size(row_axis)
+    piece_next = axis_index(row_axis)
+    before, v_now = (block_out, piece_next)
+    frame_out, e_now = (packet[None], 1)
+    while e_now < before:
+        state_next = tuple(((dd, dd ^ e_now) for dd in range(before)))
+        finding = ppermute(frame_out, row_axis, state_next)
+        y2 = v_now & e_now == 0
+        passed = jnp.where(y2, frame_out, finding)
+        value_now = jnp.where(y2, finding, frame_out)
+        frame_out = jnp.concatenate([passed, value_now])
+        e_now *= 2
+    return frame_out
 
 
 def contract_last(left_op, right_op):
@@ -149,6 +172,10 @@
     cotangent,
 ):
     local_rows = emb.shape[0]
+
+    def divide_object_by_axis(tile_in, t0, join_dim):
+        return _build_tracks(answer_masks(tile_in, t0), join_dim)
+
     query_w, key_w, value_w, out_w, router_w, gate_w, up_w, down_w = (
         lax.all_gather(w_query, "fsdp", axis=0, tiled=True),
         lax.all_gather(w_key, "fsdp", axis=0, tiled=True),
@@ -156,7 +183,7 @@
         lax.all_gather(w_out, "fsdp", axis=0, tiled=True),
         lax.all_gather(w_router, "fsdp", axis=0, tiled=True),
         lax.all_gather(w_gate, "fsdp", axis=1, tiled=True),
-        lax.all_gather(w_up, "fsdp", axis=1, tiled=True),
+        divide_object_by_axis(w_up, "fsdp", 1),
         lax.all_gather(w_down, "fsdp", axis=1, tiled=True),
     )
     gain_one = norm1_gain.astype(jnp.float32)

time: 2880 us -> 2980 us (1.035)
  blocking collectives: 90.3 us -> 348 us
  waiting for transfers between devices: 1610 us -> 1420 us
    all_gather x1, blocking collectives: 9.38 us -> 268 us  [local(): lax.all_gather(w_router, 'fsdp', axis=0, tiled=True)]
    ppermute x0 -> x3, waiting for transfers between devices: none -> 111 us  [answer_masks(): finding = ppermute(frame_out, row_axis, state_next)]
    all_gather x1 -> x0, waiting for transfers between devices: 87.2 us -> none  [local(): lax.all_gather(w_up, 'fsdp', axis=1, tiled=True)]
    all_gather x1, waiting for transfers between devices: 87.2 us -> 0.02 us  [local(): lax.all_gather(w_down, 'fsdp', axis=1, tiled=True)]
    all_gather x1, waiting for transfers between devices: 85.7 us -> 0.02 us  [local(): lax.all_gather(w_gate, 'fsdp', axis=1, tiled=True)]
    all_gather x1, waiting for transfers between devices: 34.2 us -> 0.02 us  [local(): lax.all_gather(normed_low, 'tp', axis=0, tiled=True)]
  transfers between devices with their start and end apart: 22 -> 24, of which waited for: 21 -> 19; matrix products, arithmetic and copies ran while one was open for 21% -> 22% of each run, Pallas kernels for 0% -> 0%
where the time goes in v1:
time: 2980 us; the launch traced here: 2970 us
  waiting for transfers between devices  1420 us (48%)
  other arithmetic  437 us (15%)
  matrix products  385 us (13%)
  local copies, waits for them, and re-layouts  354 us (12%)
  blocking collectives  348 us (12%)
    all_gather x1, blocking collectives, local(): lax.all_gather(w_router, 'fsdp', axis=0, tiled=True)  268 us
    reduce_scatter x1, waiting for transfers between devices, local(): lax.psum_scatter(down_grads, 'fsdp', scatter_dimension=1, tiled=True)  190 us
    reduce_scatter x1, waiting for transfers between devices, local(): lax.psum_scatter(up_grads, 'fsdp', scatter_dimension=1, tiled=True)  190 us
    reduce_scatter x1, waiting for transfers between devices, local(): lax.psum_scatter(gate_grads, 'fsdp', scatter_dimension=1, tiled=True)  190 us
    dot_general x35, matrix products, contract_last(): lax.dot_general(left_op, right_op, (((1,), (1,)), ((), ())), preferred_el...  122 us
    dot_general x35, matrix products, contract_first(): lax.dot_general(left_op, right_op, (((0,), (0,)), ((), ())), preferred_el...  117 us
    scatter-add x10, other arithmetic, expert_forward(): running = running.at[slot_rows].add(expert_out * slot_scale[:, None])  112 us
    reduce_scatter x1, waiting for transfers between devices, local(): lax.psum_scatter(total_grad + contract_last(value_proj_grad, value_w), 't...  112 us
  transfers between devices with their start and end apart: 24, of which 19 were waited for; matrix products, arithmetic and copies ran while one was open for 22% of the time, Pallas kernels for 0%

profile of v1, /device:TPU:0, one launch (start us, length us, event | category | flops | bytes accessed | tf_op | source)
XLA Modules:
  0.0 2969.4 jit_solution(7343814497067190750)
XLA Ops:
  37.2 41.9 %all-gather.10.cloned.1.call-done = bf16[1024,1536]{1,0:T(8,128)(2,1)} async-done(((bf16[256,1536]{1,0:T(8,128)(2,1)}), bf16[1024,1536]{1,0:T(8,128)(2,1)}) %all-gather.10.cloned.1.call-update) | async-done | bytes 3145744 | tf_op jit(solution)/shard_map/all_gather | solution.py:193
  89.1 14.5 all-gather.12.cloned.1.call-done
  108.4 13.1 while.70
  136.2 110.3 %reduce-scatter.13.cloned.1.call-done = f32[256,1536]{1,0:T(8,128)} async-done(((f32[1024,1536]{1,0:T(8,128)}), f32[256,1536]{1,0:T(8,128)}) %reduce-scatter.13.cloned.1.call-update) | async-done | bytes 1572880 | tf_op jit(solution)/shard_map/reduce_scatter | solution.py:215
  262.8 107.0 %collective-permute-done.1 = bf16[2,10,192,512]{3,2,1,0:T(8,128)(2,1)} collective-permute-done((bf16[2,10,192,512]{3,2,1,0:T(8,128)(2,1)}, bf16[2,10,192,512]{3,2,1,0:T(8,128)(2,1)}, u32[]{:S(2)}, u32[]{:S(2)}) %collective-permute-start.1) | collective-permute-done | bytes 3932192 | tf_op jit(solution)/shard_map/ppermute | solution.py:30
  386.7 268.1 %all-gather = bf16[8,192,40]{1,2,0:T(8,128)(2,1)S(1)} all-gather(bf16[1,192,40]{1,2,0:T(8,128)(2,1)S(1)} %bitcast.441), channel_id=1, replica_groups=mesh['fsdp'=8,'tp'=4] {'fsdp'}, dimensions={0}, use_global_device_ids=true | all-gather | bytes 138240 | tf_op jit(solution)/shard_map/all_gather | solution.py:184
  671.7 13.2 all_gather.45
  688.7 466.2 %while.71 = (s32[]{:T(128)}, f32[1024,1536]{1,0:T(8,128)}, s32[10,408]{1,0:T(8,128)}, f32[10,408]{1,0:T(8,128)}, f32[10,408,8]{2,1,0:T(8,128)}, /*index=5*/f32[1...) while((s32[]{:T(128)}, f32[1024,1536]{1,0:T(8,128)}, ...), condition=%wide.region_18.20_spmd, body=%wide.region_10.19_spmd.sunk | while | flops 1929139968 | bytes 35207396 | solution.py:250
  724.3 11.2 scatter_custom_fusion.17
  770.9 11.2 scatter_custom_fusion.17
  817.5 11.2 scatter_custom_fusion.17
  864.0 11.2 scatter_custom_fusion.17
  910.7 11.2 scatter_custom_fusion.17
  957.2 11.2 scatter_custom_fusion.17
  1159.1 504.9 %while.72 = (s32[]{:T(128)}, f32[1024,1536]{1,0:T(8,128)}, f32[1024,8]{1,0:T(8,128)}, f32[10,1536,512]{2,1,0:T(8,128)}, f32[10,1536,512]{2,1,0:T(8,128)}, /*inde...) while((s32[]{:T(128)}, f32[1024,1536]{1,0:T(8,128)}, ...), condition=%wide.region_24.26_spmd, body=%wide.region_20.25_spmd.sunk | while | flops 3863125760 | bytes 57883772 | solution.py:294
  1666.5 18.7 reduce-scatter.19.cloned.1.call-done
  1686.7 109.6 %reduce-scatter.17.cloned.1.call-done = f32[256,1536]{1,0:T(8,128)} async-done(((f32[1024,1536]{1,0:T(8,128)}), f32[256,1536]{1,0:T(8,128)}) %reduce-scatter.17.cloned.1.call-update) | async-done | bytes 1572880 | tf_op jit(solution)/shard_map/reduce_scatter | solution.py:298
  1802.2 63.0 %all-gather.24.cloned.1.call-done = bf16[1024,1536]{1,0:T(8,128)(2,1)} async-done(((bf16[256,1536]{1,0:T(8,128)(2,1)}), bf16[1024,1536]{1,0:T(8,128)(2,1)}) %all-gather.24.cloned.1.call-update) | async-done | bytes 3145744 | tf_op jit(solution)/shard_map/all_gather | solution.py:309
  1870.0 65.1 %while.73 = (s32[]{:T(128)}, f32[2,512,6,64]{1,0,3,2:T(2,128)}, f32[2,512,2,64]{1,0,3,2:T(2,128)}, bf16[2,512,2,64]{1,3,2,0:T(8,128)(2,1)}, bf16[2,512,2,64]{1,3...) while((s32[]{:T(128)}, f32[2,512,6,64]{1,0,3,2:T(2,128)}, ...), condition=%wide.region_32.34_spmd, body=%wide.region_30.33_spmd.sunk | while | flops 1031271424 | bytes 58161316 | solution.py:314
  1887.6 15.0 dynamic_update_slice.116
  1920.1 15.0 dynamic_update_slice.116
  1967.6 26.9 all-reduce.3.cloned.1.call-done
  1996.0 111.9 %reduce-scatter.21.cloned.1.call-done = f32[256,1536]{1,0:T(8,128)} async-done(((f32[1024,1536]{1,0:T(8,128)}), f32[256,1536]{1,0:T(8,128)}) %reduce-scatter.21.cloned.1.call-update) | async-done | bytes 1572880 | tf_op jit(solution)/shard_map/reduce_scatter | solution.py:341
  2109.8 45.1 %all-reduce = (f32[1536]{0:T(1024)}, f32[1536]{0:T(1024)}) all-reduce(f32[1536]{0:T(1024)S(1)} %get-tuple-element.575, f32[1536]{0:T(1024)S(1)} %get-tuple-element.573), channel_id=1, replica_groups=mesh['fsdp'=8,'tp'=4] {'fsdp','tp'}, use_global_device_ids=true, to_apply=%region_36.38 | all-reduce | flops 3072 | bytes 24576 | tf_op jit(solution)/shard_map/psum | solution.py:346
  2154.9 67.5 %reduce-scatter.15.cloned.1.call-done = f32[256,1536]{1,0:T(8,128)} async-done(((f32[1024,1536]{1,0:T(8,128)}), f32[256,1536]{1,0:T(8,128)}) %reduce-scatter.15.cloned.1.call-update) | async-done | bytes 1572880 | tf_op jit(solution)/shard_map/reduce_scatter | solution.py:251
  2227.0 34.4 %reduce-scatter.25.cloned.1.call-done = f32[192,128]{1,0:T(8,128)} async-done(((f32[1536,128]{1,0:T(8,128)}), f32[192,128]{1,0:T(8,128)}) %reduce-scatter.25.cloned.1.call-update) | async-done | bytes 98320 | tf_op jit(solution)/shard_map/reduce_scatter | solution.py:355
  2261.4 38.6 %reduce-scatter.27.cloned.1.call-done = f32[192,128]{1,0:T(8,128)} async-done(((f32[1536,128]{1,0:T(8,128)}), f32[192,128]{1,0:T(8,128)}) %reduce-scatter.27.cloned.1.call-update) | async-done | bytes 98320 | tf_op jit(solution)/shard_map/reduce_scatter | solution.py:356
  2300.0 46.1 %reduce-scatter.29.cloned.1.call-done = f32[192,384]{1,0:T(8,128)} async-done(((f32[1536,384]{1,0:T(8,128)}), f32[192,384]{1,0:T(8,128)}) %reduce-scatter.29.cloned.1.call-update) | async-done | bytes 294928 | tf_op jit(solution)/shard_map/reduce_scatter | solution.py:357
  2346.1 46.2 %reduce-scatter.23.cloned.1.call-done = f32[192,384]{1,0:T(8,128)} async-done(((f32[1536,384]{1,0:T(8,128)}), f32[192,384]{1,0:T(8,128)}) %reduce-scatter.23.cloned.1.call-update) | async-done | bytes 294928 | tf_op jit(solution)/shard_map/reduce_scatter | solution.py:354
  2392.3 190.1 %reduce-scatter.35.cloned.1.call-done = f32[10,192,512]{2,1,0:T(8,128)} async-done(((f32[10,1536,512]{2,1,0:T(8,128)}), f32[10,192,512]{2,1,0:T(8,128)}) %reduce-scatter.35.cloned.1.call-update) | async-done | bytes 3932176 | tf_op jit(solution)/shard_map/reduce_scatter | solution.py:362
  2582.4 189.9 %reduce-scatter.31.cloned.1.call-done = f32[10,192,512]{2,1,0:T(8,128)} async-done(((f32[10,1536,512]{2,1,0:T(8,128)}), f32[10,192,512]{2,1,0:T(8,128)}) %reduce-scatter.31.cloned.1.call-update) | async-done | bytes 3932176 | tf_op jit(solution)/shard_map/reduce_scatter | solution.py:360
  2772.3 190.1 %reduce-scatter.33.cloned.1.call-done = f32[10,192,512]{2,1,0:T(8,128)} async-done(((f32[10,1536,512]{2,1,0:T(8,128)}), f32[10,192,512]{2,1,0:T(8,128)}) %reduce-scatter.33.cloned.1.call-update) | async-done | bytes 3932176 | tf_op jit(solution)/shard_map/reduce_scatter | solution.py:361
  (958 shorter events, 1121.7 us)
Async XLA Ops:
  7.2 72.0 %all-gather.10.cloned.1.call-start = ((), (), s32[]{:S(2)}) async-start(), calls=%async_computation.12 | async-start | bytes 3932160 | tf_op jit(solution)/shard_map/all_gather | solution.py:193
  12.8 90.8 %all-gather.12.cloned.1.call-start = ((), (), s32[]{:S(2)}) async-start(), calls=%async_computation.13 | async-start | bytes 1327104 | tf_op jit(solution)/shard_map/all_gather | solution.py:180
  13.6 115.9 %all-gather.14.cloned.1.call-start = ((), (), s32[]{:S(2)}) async-start(), calls=%async_computation.14 | async-start | bytes 1327104 | tf_op jit(solution)/shard_map/all_gather | solution.py:183
  14.3 232.2 %reduce-scatter.13.cloned.1.call-start = ((), (), s32[]{:S(2)}) async-start(), calls=%async_computation.15 | async-start | bytes 7864320 | tf_op jit(solution)/shard_map/reduce_scatter | solution.py:215
  135.6 549.6 %all-gather.16.cloned.1.call-start = ((), (), s32[]{:S(2)}) async-start(), calls=%async_computation.16 | async-start | bytes 3932160 | tf_op jit(solution)/shard_map/all_gather | solution.py:231
  250.5 434.7 %all-gather.18.cloned.1.call-start = ((), (), s32[]{:S(2)}) async-start(), calls=%async_computation.17 | async-start | bytes 17694720 | tf_op jit(solution)/shard_map/all_gather | solution.py:185
  251.1 434.1 %all-gather.20.cloned.1.call-start = ((), (), s32[]{:S(2)}) async-start(), calls=%async_computation.18 | async-start | bytes 17694720 | tf_op jit(solution)/shard_map/all_gather | solution.py:187
  251.9 903.0 %all-gather.22.cloned.1.call-start = ((), (), s32[]{:S(2)}) async-start(), calls=%async_computation.20 | async-start | bytes 3932160 | tf_op jit(solution)/shard_map/all_gather | solution.py:255
  252.1 4.2 collective-permute-start
  261.5 108.3 %collective-permute-start.1 = (bf16[2,10,192,512]{3,2,1,0:T(8,128)(2,1)}, bf16[2,10,192,512]{3,2,1,0:T(8,128)(2,1)}, u32[]{:S(2)}, u32[]{:S(2)}) collective-permute-start(bf16[2,10,192,512]{3,2,1,0:T(8,128)(2,1)} %pad_maximum_fusion.1), channel_id=1, source_target_pairs={{0,8},{4,12},{8,0},{12,4},{16,24},{20,28},{24,16},{28,20},{1,9},{5... | collective-permute-start | bytes 11796488 | tf_op jit(solution)/shard_map/ppermute | solution.py:30
  384.1 270.9 %copy-start.56 = (s32[1024,8]{0,1:T(8,128)S(1)}, s32[1024,8]{0,1:T(8,128)}, u32[]{:S(2)}) copy-start(s32[1024,8]{0,1:T(8,128)} %param.26) | copy-start | bytes 98308
  384.1 272.0 %collective-permute-start.2 = (bf16[4,10,192,512]{3,2,1,0:T(8,128)(2,1)}, bf16[4,10,192,512]{3,2,1,0:T(8,128)(2,1)}, u32[]{:S(2)}, u32[]{:S(2)}) collective-permute-start(bf16[4,10,192,512]{3,2,1,0:T(8,128)(2,1)} %pad_maximum_fusion), channel_id=1, source_target_pairs={{0,16},{4,20},{8,24},{12,28},{16,0},{20,4},{24,8},{28,12},{1,17},{... | collective-permute-start | bytes 23592968 | tf_op jit(solution)/shard_map/ppermute | solution.py:30
  386.5 1298.7 %reduce-scatter.19.cloned.1.call-start = ((), (), s32[]{:S(2)}) async-start(), calls=%async_computation.22 | async-start | bytes 40960 | tf_op jit(solution)/shard_map/reduce_scatter | solution.py:299
  1665.8 130.5 %reduce-scatter.17.cloned.1.call-start = ((), (), s32[]{:S(2)}) async-start(), calls=%async_computation.21 | async-start | bytes 7864320 | tf_op jit(solution)/shard_map/reduce_scatter | solution.py:298
  1666.4 133.1 %copy-start.22 = (bf16[256,1536]{1,0:T(8,128)(2,1)S(1)}, bf16[256,1536]{1,0:T(8,128)(2,1)}, u32[]{:S(2)}) copy-start(bf16[256,1536]{1,0:T(8,128)(2,1)} %param.37) | copy-start | bytes 2359300
  1666.4 198.7 %all-gather.24.cloned.1.call-start = ((), (), s32[]{:S(2)}) async-start(), calls=%async_computation.23 | async-start | bytes 3932160 | tf_op jit(solution)/shard_map/all_gather | solution.py:309
  1801.0 193.4 %all-reduce.3.cloned.1.call-start = ((), (), s32[]{:S(2)}) async-start(), calls=%async_computation.29 | async-start | bytes 491520 | tf_op jit(solution)/shard_map/psum | solution.py:346
  1802.1 305.7 %reduce-scatter.21.cloned.1.call-start = ((), (), s32[]{:S(2)}) async-start(), calls=%async_computation.24 | async-start | bytes 7864320 | tf_op jit(solution)/shard_map/reduce_scatter | solution.py:341
  1948.8 273.6 %reduce-scatter.15.cloned.1.call-start = ((), (), s32[]{:S(2)}) async-start(), calls=%async_computation.19 | async-start | bytes 7864320 | tf_op jit(solution)/shard_map/reduce_scatter | solution.py:251
  1949.4 312.0 %reduce-scatter.25.cloned.1.call-start = ((), (), s32[]{:S(2)}) async-start(), calls=%async_computation.26 | async-start | bytes 884736 | tf_op jit(solution)/shard_map/reduce_scatter | solution.py:355
  1952.7 347.3 %reduce-scatter.27.cloned.1.call-start = ((), (), s32[]{:S(2)}) async-start(), calls=%async_computation.27 | async-start | bytes 884736 | tf_op jit(solution)/shard_map/reduce_scatter | solution.py:356
  1955.6 390.5 %reduce-scatter.29.cloned.1.call-start = ((), (), s32[]{:S(2)}) async-start(), calls=%async_computation.28 | async-start | bytes 2654208 | tf_op jit(solution)/shard_map/reduce_scatter | solution.py:357
  1961.0 431.3 %reduce-scatter.23.cloned.1.call-start = ((), (), s32[]{:S(2)}) async-start(), calls=%async_computation.25 | async-start | bytes 2654208 | tf_op jit(solution)/shard_map/reduce_scatter | solution.py:354
  1965.5 616.9 %reduce-scatter.35.cloned.1.call-start = ((), (), s32[]{:S(2)}) async-start(), calls=%async_computation.32 | async-start | bytes 35389440 | tf_op jit(solution)/shard_map/reduce_scatter | solution.py:362
  1966.2 806.0 %reduce-scatter.31.cloned.1.call-start = ((), (), s32[]{:S(2)}) async-start(), calls=%async_computation.30 | async-start | bytes 35389440 | tf_op jit(solution)/shard_map/reduce_scatter | solution.py:360
  1966.8 995.5 %reduce-scatter.33.cloned.1.call-start = ((), (), s32[]{:S(2)}) async-start(), calls=%async_computation.31 | async-start | bytes 35389440 | tf_op jit(solution)/shard_map/reduce_scatter | solution.py:361
  1966.9 141.0 %copy-start.13 = (bf16[256,1536]{1,0:T(8,128)(2,1)S(1)}, bf16[256,1536]{1,0:T(8,128)(2,1)}, u32[]{:S(2)}) copy-start(bf16[256,1536]{1,0:T(8,128)(2,1)} %param.24) | copy-start | bytes 2359300
  1966.9 141.0 %copy-start.51 = (f32[1536]{0:T(1024)S(1)}, f32[1536]{0:T(1024)}, u32[]{:S(2)}) copy-start(f32[1536]{0:T(1024)} %copy-done.50) | copy-start | bytes 18436
  1966.9 141.0 %copy-start.67 = (f32[256]{0:T(256)S(1)}, f32[256]{0:T(256)}, u32[]{:S(2)}) copy-start(f32[256]{0:T(256)} %copy-done.66) | copy-start | bytes 3076
  1966.9 255.5 %copy-start.69 = (f32[256]{0:T(256)S(1)}, f32[256]{0:T(256)}, u32[]{:S(2)}) copy-start(f32[256]{0:T(256)} %get-tuple-element.721) | copy-start | bytes 3076
  1967.6 254.8 %copy-start.5 = (f32[256,1536]{1,0:T(8,128)S(1)}, f32[256,1536]{1,0:T(8,128)}, u32[]{:S(2)}) copy-start(f32[256,1536]{1,0:T(8,128)} %copy-done.3) | copy-start | bytes 4718596
  1967.6 254.8 %copy-start.23 = (bf16[256,1536]{1,0:T(8,128)(2,1)S(1)}, bf16[256,1536]{1,0:T(8,128)(2,1)}, u32[]{:S(2)}) copy-start(bf16[256,1536]{1,0:T(8,128)(2,1)} %param.37) | copy-start | bytes 2359300
  (157 other events, 1808.3 us)
Sparse Core Ops, SparseCore 0:
  12.9 66.1 all-gather.9
  81.0 22.5 all-gather.11
  105.5 23.9 all-gather.13
  135.7 110.7 reduce-scatter.12
  250.7 63.9 all-gather.15
  316.4 136.5 all-gather.17
  454.9 149.6 all-gather.19
  606.2 63.4 all-gather.21
  1666.0 19.2 reduce-scatter.18
  1687.4 108.9 reduce-scatter.16
  1801.2 63.9 all-gather.23
  1870.5 123.9 all-reduce.2
  1996.8 111.0 reduce-scatter.20
  2110.0 112.3 reduce-scatter.14
  2226.0 35.4 reduce-scatter.24
  2265.0 34.9 reduce-scatter.26
  2303.8 42.3 reduce-scatter.28
  2349.9 42.3 reduce-scatter.22
  2396.5 185.8 reduce-scatter.34
  2586.4 185.8 reduce-scatter.30
  2776.5 185.8 reduce-scatter.32
